TPU v7x, 32 devices: a whole 2x2x4 slice. The times are simulated.
32 devices in a mesh: dp: 8 (over z, y), mp: 4 (over x, core).
Axes of the slice: x: 2, y: 2, z: 4, core: 2. Of those that a mesh axis runs over, the one named last changes fastest.
Arguments:
- slow_weights: float32 [1, 3584, 1024], P(None, None, 'mp'), may hold values from -6 to 6
- fast_weights: bfloat16 [8, 1, 3584, 1024], P('dp', None, None, 'mp'), may hold values from -64 to 64
- momentum: float32 [1, 3584, 1024], P(None, None, 'mp'), may hold values from -1.2 to 1.2
Outputs:
- slow_next: float32 [1, 3584, 1024], P(None, None, 'mp')
- momentum_next: float32 [1, 3584, 1024], P(None, None, 'mp')
- fast_next: bfloat16 [8, 1, 3584, 1024], P('dp', None, None, 'mp')
All inputs are finite; a program needn't handle non-finite values.
Results may differ from a plain program's by a relative error of at most 0.001.
Values sent between devices are 32-bit elements; how exact they have to be, the bound alone decides.
A program may use at most 64 MiB of HBM per device.

v0:
```python
import functools
import math

import jax
import jax.numpy as jnp
from jax import lax
from jax.experimental import pallas as pl
from jax.experimental.pallas import tpu as pltpu
from jax.sharding import PartitionSpec as P

MOMENTUM_RATE = 0.9
OUTER_RATE = 0.7
CLIP_LEVEL = 0.2
EPSILON = 1e-06
MESH = pl.DeviceIdType.MESH
SUBS = 4
VMEM_LIMIT = 24 * 1024 * 1024


def device_at(place, n):
    half = n // 2
    up = 2 * place
    down = 2 * (n - 1 - place) + 1
    return jnp.where(place < half, up, down)


def kernel(n, m, subs, max_norm, slow_hbm, fast_hbm, moment_hbm,
           slow_out, moment_out, fast_out,
           ring, slow_ref, fast_ref, moment_ref, pseudo_ref, parts, norms, moment_sem, load_sem, send_sem, recv_sem,
           part_send, part_recv, norm_send, norm_recv):
    rows, cols = slow_ref.shape
    chunk = rows // n
    sub = chunk // subs
    half = cols // 2
    me = lax.axis_index("dp")
    mine = lax.axis_index("mp")
    z, y = me // 2, lax.rem(me, 2)
    place = jnp.where(y == 0, z, n - 1 - z)
    right = device_at(lax.rem(place + 1, n), n)
    left = device_at(lax.rem(place + n - 1, n), n)
    goal = (right, left)
    order = (place, lax.rem(n - place, n))

    def load(d, k):
        c = lax.rem(order[d] - k + n, n)
        at = (pl.ds(pl.multiple_of(c * chunk, chunk), chunk), pl.ds(d * half, half))
        return (
            pltpu.make_async_copy(slow_hbm.at[at], slow_ref.at[at], load_sem.at[0, d, k]),
            pltpu.make_async_copy(fast_hbm.at[at], fast_ref.at[at], load_sem.at[1, d, k]),
        )

    for d in range(2):
        for copy in load(d, 0):
            copy.start()
    barrier = pltpu.get_barrier_semaphore()
    for other in (left, right):
        pl.semaphore_signal(barrier, inc=1, device_id={"dp": other}, device_id_type=MESH)
    for k in range(1, m):
        pl.semaphore_signal(
            barrier, inc=1, device_id={"mp": lax.rem(mine + k, m)}, device_id_type=MESH
        )
    moment_load = pltpu.make_async_copy(moment_hbm, moment_ref, moment_sem)

    def start_row(c, b):
        return pl.multiple_of(c * chunk + b * sub, sub)

    def own(d, b, c):
        at = (pl.ds(start_row(c, b), sub), pl.ds(d * half, half))
        return slow_ref[at] - fast_ref[at].astype(jnp.float32)

    def reduce_copy(d, b, s):
        return pltpu.make_async_remote_copy(
            src_ref=ring.at[d, b, s], dst_ref=ring.at[d, b, s + 1],
            send_sem=send_sem.at[d, b, s], recv_sem=recv_sem.at[d, b, s],
            device_id={"dp": goal[d]}, device_id_type=MESH,
        )

    def gather_copy(d, b, s, c):
        at = (pl.ds(start_row(c, b), sub), pl.ds(d * half, half))
        return pltpu.make_async_remote_copy(
            src_ref=pseudo_ref.at[at], dst_ref=pseudo_ref.at[at],
            send_sem=send_sem.at[d, b, n - 1 + s], recv_sem=recv_sem.at[d, b, n - 1 + s],
            device_id={"dp": goal[d]}, device_id_type=MESH,
        )

    def part_copy(k):
        return pltpu.make_async_remote_copy(
            src_ref=parts.at[me], dst_ref=parts.at[me],
            send_sem=part_send.at[k], recv_sem=part_recv.at[k],
            device_id={"dp": lax.rem(me + k, n)}, device_id_type=MESH,
        )

    def norm_copy(k):
        return pltpu.make_async_remote_copy(
            src_ref=norms.at[mine], dst_ref=norms.at[mine],
            send_sem=norm_send.at[k], recv_sem=norm_recv.at[k],
            device_id={"mp": lax.rem(mine + k, m)}, device_id_type=MESH,
        )

    streams = [(d, b) for b in range(subs) for d in range(2)]
    for k in range(1, n):
        for d in range(2):
            for copy in load(d, k):
                copy.start()
    for d in range(2):
        for copy in load(d, 0):
            copy.wait()
    pl.semaphore_wait(barrier, 2 + m - 1)
    for d, b in streams:
        ring[d, b, 0] = own(d, b, order[d])
        reduce_copy(d, b, 0).start()
    moment_load.start()

    def reduce_step(s, carry):
        for d in range(2):
            for copy in load(d, s + 1):
                copy.wait()
        for d, b in streams:
            c = lax.rem(order[d] - s - 1 + n, n)
            reduce_copy(d, b, s).wait_recv()
            ring[d, b, s + 1] = ring[d, b, s + 1] + own(d, b, c)
            reduce_copy(d, b, s + 1).start()
        return carry

    lax.fori_loop(0, n - 2, reduce_step, 0)
    for d in range(2):
        for copy in load(d, n - 1):
            copy.wait()
    part = jnp.zeros((8, half), jnp.float32)
    for d, b in streams:
        c = lax.rem(order[d] + 1, n)
        reduce_copy(d, b, n - 2).wait_recv()
        value = (ring[d, b, n - 1] + own(d, b, c)) / n
        pseudo_ref[pl.ds(start_row(c, b), sub), pl.ds(d * half, half)] = value
        gather_copy(d, b, 0, c).start()
        part = part + jnp.sum((value * value).reshape(sub // 8, 8, half), axis=0)
    parts[me] = part

    def gather_step(s, carry):
        for d, b in streams:
            c = lax.rem(order[d] - s + n, n)
            gather_copy(d, b, s, c).wait_recv()
            gather_copy(d, b, s + 1, c).start()
        return carry

    second = (n - 2) // 2
    first = second // 2
    for k in range(1, n):
        part_copy(k).start()
    lax.fori_loop(0, first, gather_step, 0)
    for k in range(1, n):
        part_copy(k).wait_recv()
    norm = parts[0]
    for j in range(1, n):
        norm = norm + parts[j]
    norms[mine] = norm
    for k in range(1, m):
        norm_copy(k).start()
    lax.fori_loop(first, second, gather_step, 0)
    for k in range(1, m):
        norm_copy(k).wait_recv()
    total = norms[0]
    for j in range(1, m):
        total = total + norms[j]
    total = jnp.sum(jnp.sum(total, axis=1, keepdims=True), axis=0, keepdims=True)
    factor = jnp.minimum(1.0, max_norm / (jnp.sqrt(total) + EPSILON))
    moment_load.wait()

    def update(d, c, start=0, size=chunk):
        at = (pl.ds(pl.multiple_of(c * chunk + start, 16), size), pl.ds(d * half, half))
        gradient = factor * pseudo_ref[at]
        moment = MOMENTUM_RATE * moment_ref[at] + gradient
        slow = slow_ref[at] - OUTER_RATE * (gradient + MOMENTUM_RATE * moment)
        moment_out[at] = moment
        slow_out[at] = slow
        fast_out[at] = slow.astype(fast_out.dtype)

    def update_step(s, carry):
        gather_step(s, carry)
        for d in range(2):
            update(d, lax.rem(order[d] - s + n, n))
            update(d, lax.rem(order[d] - (s - second) + n, n))
        return carry

    lax.fori_loop(second, n - 2, update_step, 0)
    for d in range(2):
        update(d, lax.rem(order[d] + 1, n))
    for k in range(1, n):
        part_copy(k).wait_send()
    for k in range(1, m):
        norm_copy(k).wait_send()

    def drain(s, carry):
        for d, b in streams:
            reduce_copy(d, b, s).wait_send()
            gather_copy(d, b, s, 0).wait_send()
        return carry

    lax.fori_loop(0, n - 2, drain, 0)
    for d, b in streams:
        c = lax.rem(order[d] + 2, n)
        reduce_copy(d, b, n - 2).wait_send()
        gather_copy(d, b, n - 2, c).wait()
        update(d, c, b * sub, sub)


def emit_kernel(pieces, *refs):
    count = len(refs) // 2
    sources, targets, sem = refs[:count], refs[count:-1], refs[-1]
    size = sources[0].shape[0] // pieces
    copies = [
        pltpu.make_async_copy(
            sources[i].at[pl.ds(k * size, size)], targets[i].at[pl.ds(k * size, size)], sem.at[i, k]
        )
        for k in range(pieces) for i in range(count)
    ]
    for copy in copies:
        copy.start()
    for copy in copies:
        copy.wait()


def emit(arrays, pieces):
    return pl.pallas_call(
        functools.partial(emit_kernel, pieces),
        out_shape=tuple(jax.ShapeDtypeStruct(x.shape, x.dtype) for x in arrays),
        in_specs=[pl.BlockSpec(memory_space=pltpu.VMEM)] * len(arrays),
        out_specs=tuple(pl.BlockSpec(memory_space=pltpu.HBM) for _ in arrays),
        scratch_shapes=[pltpu.SemaphoreType.DMA((len(arrays), pieces))],
        compiler_params=pltpu.CompilerParams(vmem_limit_bytes=VMEM_LIMIT),
        name="emit",
    )(*arrays)


def body(slow_weights, fast_weights, momentum):
    n, m = lax.axis_size("dp"), lax.axis_size("mp")
    layers, depth, cols = slow_weights.shape
    rows = layers * depth
    max_norm = CLIP_LEVEL * math.sqrt(rows * cols * m)
    subs = SUBS
    while rows % (n * subs * 16):
        subs -= 1
    sub = rows // (n * subs)
    slow = slow_weights.reshape(rows, cols)
    hbm = pl.BlockSpec(memory_space=pltpu.HBM)
    vmem = pl.BlockSpec(memory_space=pltpu.VMEM)
    flat = (slow_weights, fast_weights, momentum)
    flat = [
        pltpu.with_memory_space_constraint(x.reshape(rows, cols), pltpu.HBM) for x in flat
    ]
    results = pl.pallas_call(
        functools.partial(kernel, n, m, subs, max_norm),
        out_shape=(
            jax.ShapeDtypeStruct((rows, cols), jnp.float32),
            jax.ShapeDtypeStruct((rows, cols), jnp.float32),
            jax.ShapeDtypeStruct((rows, cols), jnp.bfloat16),
        ),
        in_specs=[hbm, hbm, hbm],
        out_specs=(vmem, vmem, vmem),
        scratch_shapes=[
            pltpu.VMEM((2, subs, n, sub, cols // 2), jnp.float32),
            pltpu.VMEM((rows, cols), jnp.float32),
            pltpu.VMEM((rows, cols), jnp.bfloat16),
            pltpu.VMEM((rows, cols), jnp.float32),
            pltpu.VMEM((rows, cols), jnp.float32),
            pltpu.VMEM((n, 8, cols // 2), jnp.float32),
            pltpu.VMEM((m, 8, cols // 2), jnp.float32),
            pltpu.SemaphoreType.DMA,
            pltpu.SemaphoreType.DMA((2, 2, n)),
            pltpu.SemaphoreType.DMA((2, subs, 2 * n - 2)),
            pltpu.SemaphoreType.DMA((2, subs, 2 * n - 2)),
            pltpu.SemaphoreType.DMA((n,)),
            pltpu.SemaphoreType.DMA((n,)),
            pltpu.SemaphoreType.DMA((m,)),
            pltpu.SemaphoreType.DMA((m,)),
        ],
        compiler_params=pltpu.CompilerParams(
            collective_id=0, has_side_effects=True, vmem_limit_bytes=VMEM_LIMIT
        ),
        name="ring",
    )(*flat)
    slow_next, momentum_next, fast_next = emit(results, 4)
    return (
        slow_next.reshape(slow_weights.shape),
        momentum_next.reshape(slow_weights.shape),
        fast_next.reshape(fast_weights.shape),
    )


def solution(mesh):
    in_specs = (P(None, None, "mp"), P("dp", None, None, "mp"), P(None, None, "mp"))
    out_specs = (P(None, None, "mp"), P(None, None, "mp"), P("dp", None, None, "mp"))
    return jax.shard_map(body, mesh=mesh, in_specs=in_specs, out_specs=out_specs, check_vma=False)
```

profile of v0, /device:TPU:0, one launch (start us, length us, event | category | flops | bytes accessed | tf_op | source)
XLA Modules:
  0.0 81.7 jit_solution(1748748784282840822)
XLA Ops:
  0.6 77.5 %ring.1 = (f32[3584,256]{1,0:T(8,128)S(1)}, f32[3584,256]{1,0:T(8,128)S(1)}, bf16[3584,256]{1,0:T(8,128)(2,1)S(1)}) custom-call(f32[3584,256]{1,0:T(8,128)} %bitcast.6, bf16[3584,256]{1,0:T(8,128)(2,1)} %bitcast.8, f32[3584,256]{1,0:T(8,128)} %bitcast.7), custom_call_target="tpu_custom_call" | custom-call | tf_op jit(solution)/shard_map/ring/pallas_call | solution.py:251
  78.1 3.6 %emit.1 = (f32[3584,256]{1,0:T(8,128)}, f32[3584,256]{1,0:T(8,128)}, bf16[3584,256]{1,0:T(8,128)(2,1)}) custom-call(f32[3584,256]{1,0:T(8,128)S(1)} %get-tuple-element.9.refs_0_, f32[3584,256]{1,0:T(8,128)S(1)} %get-tuple-element.10.refs_1_, bf16[3584,256]{1,0:T(8,128)(2,1)S(1)} %get-tuple-element.11.refs_2_), custom_call_target="tpu_custom_call" | custom-call | tf_op jit(solution)/shard_map/emit/pallas_call | solution.py:224
where the time goes:
time: 81.9 us; the launch traced here: 81.7 us
  Pallas kernels  81.1 us (99%)
    pallas_call x1, Pallas kernels, body(): pl.pallas_call(functools.partial(kernel, n, m, subs, max_norm), out_shape...  77.5 us
    pallas_call x1, Pallas kernels, emit(): pl.pallas_call(functools.partial(emit_kernel, pieces), out_shape=tuple((j...  3.63 us

commit v1 on v0

--- a/solution.py
+++ b/solution.py
@@ -15,6 +15,316 @@
 MESH = pl.DeviceIdType.MESH
 SUBS = 4
 VMEM_LIMIT = 24 * 1024 * 1024
+LADDER_LIMIT = 40 * 1024 * 1024
+
+OUTER = (
+    (3, 0, 1, 0), (11, 0, 4, 0), (7, 0, 4, 0), (51, 0, 1, 0), (2, 0, 1, 0), (9, 0, 4, 0),
+    (1, 0, 1, 0), (45, 0, 4, 0), (10, 4, 1, 0), (5, 1, 4, 0), (6, 4, 1, 0), (47, 1, 4, 0),
+    (0, 0, 1, 0), (41, 1, 4, 0), (8, 4, 1, 0), (53, 1, 4, 0), (4, 4, 1, 0), (43, 0, 4, 0),
+    (46, 4, 1, 0), (55, 0, 4, 0), (49, 0, 1, 0), (35, 1, 4, 0), (44, 4, 1, 0), (37, 1, 4, 0),
+    (50, 0, 1, 0), (21, 1, 4, 0), (48, 0, 1, 0), (33, 0, 4, 0), (42, 4, 1, 0), (31, 0, 4, 0),
+    (40, 4, 1, 0), (39, 0, 4, 0), (54, 4, 1, 0), (27, 1, 4, 0), (15, 0, 1, 0), (19, 0, 4, 0),
+    (34, 4, 1, 0), (23, 1, 4, 0), (52, 4, 1, 0), (29, 0, 4, 0), (32, 4, 1, 0), (6, 8, 32, 2),
+    (13, 0, 1, 0), (25, 0, 4, 0), (14, 0, 1, 0), (8, 8, 32, 2), (30, 4, 1, 0), (48, 8, 32, 2),
+    (26, 4, 1, 0), (4, 8, 32, 2), (12, 0, 1, 0), (46, 8, 32, 2), (28, 4, 1, 0), (50, 8, 32, 2),
+    (49, 8, 8, 2), (44, 8, 32, 2), (24, 4, 1, 0), (40, 8, 32, 2), (38, 4, 1, 0), (52, 8, 32, 2),
+    (22, 4, 1, 0), (42, 8, 32, 2), (18, 4, 1, 0), (54, 8, 32, 2), (17, 0, 1, 0), (34, 8, 32, 2),
+    (36, 4, 1, 0), (32, 8, 32, 2), (20, 4, 1, 0), (12, 8, 32, 2), (16, 0, 1, 0), (28, 8, 32, 2),
+    (24, 8, 32, 2), (30, 8, 32, 2), (13, 8, 8, 2), (26, 8, 32, 2), (36, 8, 32, 2), (31, 8, 8, 2),
+    (16, 8, 32, 2), (38, 8, 32, 2), (37, 8, 8, 2), (22, 8, 32, 2), (17, 8, 8, 2), (0, 8, 0, 2),
+    (2, 8, 0, 2), (1, 8, 0, 2), (10, 8, 0, 2), (3, 8, 0, 2), (11, 8, 0, 2), (7, 8, 0, 2),
+    (9, 8, 0, 2), (5, 8, 0, 2), (47, 8, 0, 2), (51, 8, 0, 2), (45, 8, 0, 2), (41, 8, 0, 2),
+    (53, 8, 0, 2), (43, 8, 0, 2), (14, 8, 0, 2), (55, 8, 0, 2), (35, 8, 0, 2), (33, 8, 0, 2),
+    (15, 8, 0, 2), (29, 8, 0, 2), (25, 8, 0, 2), (20, 8, 0, 2), (27, 8, 0, 2), (21, 8, 0, 2),
+    (39, 8, 0, 2), (18, 8, 0, 2), (23, 8, 0, 2), (19, 8, 0, 2),
+)
+INNER = (
+    (5, 0, 1, 0), (47, 0, 1, 0), (9, 0, 4, 0), (11, 0, 4, 0), (41, 0, 1, 0), (7, 0, 4, 0),
+    (53, 0, 1, 0), (45, 0, 4, 0), (3, 1, 2, 0), (35, 0, 1, 0), (43, 0, 4, 0), (51, 1, 2, 0),
+    (27, 0, 1, 0), (55, 0, 4, 0), (2, 1, 2, 0), (37, 0, 1, 0), (33, 0, 4, 0), (21, 0, 1, 0),
+    (1, 3, 4, 0), (10, 5, 2, 0), (23, 0, 1, 0), (29, 0, 4, 0), (6, 5, 2, 0), (25, 0, 4, 0),
+    (0, 3, 4, 0), (0, 4, 24, 3), (8, 7, 56, 1), (4, 3, 56, 1), (46, 1, 2, 0), (31, 0, 4, 0),
+    (2, 8, 8, 2), (1, 4, 24, 3), (49, 3, 4, 0), (10, 8, 40, 2), (50, 1, 2, 0), (6, 8, 40, 2),
+    (44, 7, 56, 1), (3, 8, 8, 2), (42, 5, 2, 0), (39, 0, 4, 0), (48, 7, 24, 1), (19, 0, 4, 0),
+    (11, 8, 8, 2), (54, 5, 2, 0), (46, 8, 40, 2), (15, 1, 2, 0), (50, 8, 40, 2), (34, 1, 2, 0),
+    (40, 3, 56, 1), (52, 3, 56, 1), (32, 7, 56, 1), (13, 3, 4, 0), (14, 1, 2, 0), (42, 8, 40, 2),
+    (30, 5, 2, 0), (54, 8, 40, 2), (26, 1, 2, 0), (34, 8, 40, 2), (12, 7, 24, 1), (28, 7, 56, 1),
+    (14, 8, 40, 2), (24, 7, 56, 1), (30, 8, 8, 2), (38, 5, 2, 0), (22, 1, 2, 0), (15, 8, 8, 2),
+    (26, 8, 40, 2), (18, 5, 2, 0), (17, 1, 4, 0), (36, 3, 24, 1), (20, 3, 56, 1), (16, 7, 24, 1),
+    (-1, 0, 0, 4), (38, 8, 40, 2), (22, 8, 40, 2), (21, 8, 8, 2), (-1, 0, 0, 5), (18, 8, 40, 2),
+    (19, 8, 8, 2), (9, 8, 0, 2), (5, 8, 0, 2), (7, 8, 0, 2), (45, 8, 0, 2), (47, 8, 0, 2),
+    (51, 8, 0, 2), (41, 8, 0, 2), (53, 8, 0, 2), (33, 8, 0, 2), (43, 8, 0, 2), (49, 8, 0, 2),
+    (55, 8, 0, 2), (35, 8, 0, 2), (29, 8, 0, 2), (25, 8, 0, 2), (27, 8, 0, 2), (13, 8, 0, 2),
+    (39, 8, 0, 2), (23, 8, 0, 2), (31, 8, 0, 2), (37, 8, 0, 2), (17, 8, 0, 2),
+)
+
+
+def ladder_kernel(n, m, max_norm, slow_hbm, fast_hbm, moment_hbm,
+                  pseudo, slow_ref, moment_ref, factor_ref,
+                  fast_ref, part, inbox, square, norms, parts,
+                  moment_sem, load_sem, send_sem, recv_sem, norm_send, norm_recv, part_send, part_recv):
+    rows, cols = slow_ref.shape
+    groups = load_sem.shape[1]
+    size = rows // (4 * groups)
+    half = n // 4
+    me = lax.axis_index("dp")
+    mine = lax.axis_index("mp")
+    z, y = me // 2, lax.rem(me, 2)
+    upper = z // half
+    step = 1 - 2 * upper
+    outer = lax.rem(z + upper, half) == 0
+    away = jnp.where(outer, step, -step)
+    near = 2 * (z + away) + y
+    across = 2 * (z + step) + y
+    rung = 2 * z + 1 - y
+    target = (near, across, rung)
+    spots = [(far + upper - 2 * far * upper) * 2 + (other + y - 2 * other * y) for far in range(2) for other in range(2)]
+    block = size * 4
+
+    def load(g):
+        at = pl.ds(g * block, block)
+        return (
+            pltpu.make_async_copy(slow_hbm.at[at], slow_ref.at[at], load_sem.at[0, g]),
+            pltpu.make_async_copy(fast_hbm.at[at], fast_ref.at[at], load_sem.at[1, g]),
+        )
+
+    loads = []
+    for entry in OUTER + INNER:
+        if entry[0] >= 0 and entry[0] // 4 not in loads:
+            loads.append(entry[0] // 4)
+    for g in loads[:2]:
+        for copy in load(g):
+            copy.start()
+    barrier = pltpu.get_barrier_semaphore()
+    for other in (near, rung):
+        pl.semaphore_signal(barrier, inc=1, device_id={"dp": other}, device_id_type=MESH)
+    for k in range(1, m):
+        pl.semaphore_signal(
+            barrier, inc=1, device_id={"mp": lax.rem(mine + k, m)}, device_id_type=MESH
+        )
+
+    @pl.when(jnp.logical_not(outer))
+    def _():
+        pl.semaphore_signal(barrier, inc=1, device_id={"dp": across}, device_id_type=MESH)
+
+    for g in loads[2:]:
+        for copy in load(g):
+            copy.start()
+    moment_load = pltpu.make_async_copy(moment_hbm, moment_ref, moment_sem)
+    moment_load.start()
+    square[...] = jnp.zeros_like(square)
+
+    def place(chunk):
+        return (chunk // 4) * 4 + spots[chunk % 4]
+
+    def at_of(spot):
+        return pl.ds(pl.multiple_of(spot * size, size), size)
+
+    def sum_copy(spot, k):
+        at = at_of(spot)
+        return pltpu.make_async_remote_copy(
+            src_ref=part.at[at], dst_ref=inbox.at[k, at], send_sem=send_sem, recv_sem=recv_sem.at[k, spot],
+            device_id={"dp": target[k]}, device_id_type=MESH,
+        )
+
+    def mean_copy(spot, k):
+        at = at_of(spot)
+        return pltpu.make_async_remote_copy(
+            src_ref=pseudo.at[at], dst_ref=pseudo.at[at], send_sem=send_sem, recv_sem=recv_sem.at[3, spot],
+            device_id={"dp": target[k]}, device_id_type=MESH,
+        )
+
+    def norm_copy(k):
+        return pltpu.make_async_remote_copy(
+            src_ref=norms.at[mine], dst_ref=norms.at[mine], send_sem=norm_send.at[k], recv_sem=norm_recv.at[k],
+            device_id={"mp": lax.rem(mine + k, m)}, device_id_type=MESH,
+        )
+
+    def part_copy(k):
+        return pltpu.make_async_remote_copy(
+            src_ref=parts.at[me], dst_ref=parts.at[me], send_sem=part_send.at[k], recv_sem=part_recv.at[me],
+            device_id={"dp": lax.rem(me + k, n)}, device_id_type=MESH,
+        )
+
+    roots = [2 * q + c for q in (half - 1, half) for c in range(2)]
+
+    def part_wait(j):
+        pltpu.make_async_remote_copy(
+            src_ref=parts.at[j], dst_ref=parts.at[j], send_sem=part_send.at[0], recv_sem=part_recv.at[j],
+            device_id={"dp": lax.rem(me + 1, n)}, device_id_type=MESH,
+        ).wait_recv()
+
+    def run(steps):
+        seen = set()
+        sent = 0
+        for chunk, waits, sends, kind in steps:
+            if kind == 4:
+                norms[mine] = square[:, : cols // 2] + square[:, cols // 2 :]
+                for k in range(1, m):
+                    norm_copy(k).start()
+                continue
+            if kind == 5:
+                for k in range(1, m):
+                    norm_copy(k).wait_recv()
+                total = norms[0]
+                for j in range(1, m):
+                    total = total + norms[j]
+                parts[me] = total
+                for k in range(1, n):
+                    part_copy(k).start()
+                continue
+            g = chunk // 4
+            if kind != 2 and g not in seen:
+                seen.add(g)
+                for copy in load(g):
+                    copy.wait()
+            spot = place(chunk)
+            at = at_of(spot)
+            for k in range(3):
+                if waits >> k & 1:
+                    sum_copy(spot, k).wait_recv()
+            if waits & 8:
+                mean_copy(spot, 2).wait_recv()
+            if kind in (0, 1, 3):
+                value = part[at] if kind == 3 else slow_ref[at] - fast_ref[at].astype(jnp.float32)
+                for k in range(3):
+                    if waits >> k & 1:
+                        value = value + inbox[k, at]
+                if kind == 0:
+                    part[at] = value
+                else:
+                    value = value * (1.0 / n)
+                    pseudo[at] = value
+            for k in (1, 0, 2):
+                if sends >> k & 1:
+                    sum_copy(spot, k).start()
+                    sent += 1
+                if sends >> (3 + k) & 1:
+                    mean_copy(spot, k).start()
+                    sent += 1
+            if kind in (1, 3):
+                weight = 1.0 if kind == 1 else 0.5
+                square[...] += weight * jnp.sum((value * value).reshape(size // 8, 8, cols), axis=0)
+        for g in loads:
+            if g not in seen:
+                for copy in load(g):
+                    copy.wait()
+        whole = inbox.reshape(3 * rows, cols).at[pl.ds(0, sent * size)]
+        pltpu.make_async_copy(whole, whole, send_sem).wait()
+
+    @pl.when(outer)
+    def _():
+        pl.semaphore_wait(barrier, m + 1)
+        run(OUTER)
+        for j in roots:
+            part_wait(j)
+
+    @pl.when(jnp.logical_not(outer))
+    def _():
+        pl.semaphore_wait(barrier, m + 2)
+        run(INNER)
+        for k in range(1, m):
+            norm_copy(k).wait_send()
+        for k in range(1, n):
+            part_copy(k).wait_send()
+        for j in roots:
+
+            @pl.when(me != j)
+            def _():
+                part_wait(j)
+
+    total = parts[roots[0]]
+    for j in roots[1:]:
+        total = total + parts[j]
+    total = jnp.sum(jnp.sum(total, axis=1, keepdims=True), axis=0, keepdims=True)
+    factor = jnp.minimum(1.0, max_norm / (jnp.sqrt(total) + EPSILON))
+    factor_ref[...] = jnp.broadcast_to(factor, factor_ref.shape)
+    moment_load.wait()
+
+
+def update_kernel(pieces, pseudo, slow_ref, moment_ref, factor_ref,
+                  slow_out, moment_out, fast_out, slow_new, moment_new, fast_new, sem):
+    rows, cols = slow_ref.shape
+    size = rows // pieces
+    factor = factor_ref[0:1, 0:1]
+
+    def copies(k):
+        at = pl.ds(pl.multiple_of(k * size, size), size)
+        pairs = ((slow_new, slow_out), (moment_new, moment_out), (fast_new, fast_out))
+        return [pltpu.make_async_copy(a.at[at], b.at[at], sem.at[i, k]) for i, (a, b) in enumerate(pairs)]
+
+    def piece(k, carry):
+        at = pl.ds(pl.multiple_of(k * size, size), size)
+        gradient = factor * pseudo[at]
+        moment = MOMENTUM_RATE * moment_ref[at] + gradient
+        slow = slow_ref[at] - OUTER_RATE * (gradient + MOMENTUM_RATE * moment)
+        moment_new[at] = moment
+        slow_new[at] = slow
+        fast_new[at] = slow.astype(fast_new.dtype)
+        for copy in copies(k):
+            copy.start()
+        return carry
+
+    def finish(k, carry):
+        for copy in copies(k):
+            copy.wait()
+        return carry
+
+    lax.fori_loop(0, pieces, piece, 0)
+    lax.fori_loop(0, pieces, finish, 0)
+
+
+def ladder(n, m, max_norm, slow, fast, moment):
+    rows, cols = slow.shape
+    groups = 1 + max(e[0] for e in OUTER + INNER) // 4
+    hbm = pl.BlockSpec(memory_space=pltpu.HBM)
+    vmem = pl.BlockSpec(memory_space=pltpu.VMEM)
+    whole = jax.ShapeDtypeStruct((rows, cols), jnp.float32)
+    dma = pltpu.SemaphoreType.DMA
+    flat = [pltpu.with_memory_space_constraint(x, pltpu.HBM) for x in (slow, fast, moment)]
+    results = pl.pallas_call(
+        functools.partial(ladder_kernel, n, m, max_norm),
+        out_shape=(whole, whole, whole, jax.ShapeDtypeStruct((8, 128), jnp.float32)),
+        in_specs=[hbm, hbm, hbm],
+        out_specs=(vmem, vmem, vmem, vmem),
+        scratch_shapes=[
+            pltpu.VMEM((rows, cols), fast.dtype),
+            pltpu.VMEM((rows, cols), jnp.float32),
+            pltpu.VMEM((3, rows, cols), jnp.float32),
+            pltpu.VMEM((8, cols), jnp.float32),
+            pltpu.VMEM((m, 8, cols // 2), jnp.float32),
+            pltpu.VMEM((n, 8, cols // 2), jnp.float32),
+            dma,
+            dma((2, groups)),
+            dma,
+            dma((4, 4 * groups)),
+            dma((m,)),
+            dma((m,)),
+            dma((n,)),
+            dma((n,)),
+        ],
+        compiler_params=pltpu.CompilerParams(
+            collective_id=0, has_side_effects=True, vmem_limit_bytes=LADDER_LIMIT
+        ),
+        name="ladder",
+    )(*flat)
+    pieces = 14
+    while rows % (pieces * 16):
+        pieces -= 1
+    return pl.pallas_call(
+        functools.partial(update_kernel, pieces),
+        out_shape=(whole, whole, jax.ShapeDtypeStruct((rows, cols), fast.dtype)),
+        in_specs=[vmem] * 4,
+        out_specs=(hbm, hbm, hbm),
+        scratch_shapes=[
+            pltpu.VMEM((rows, cols), jnp.float32),
+            pltpu.VMEM((rows, cols), jnp.float32),
+            pltpu.VMEM((rows, cols), fast.dtype),
+            dma((3, pieces)),
+        ],
+        compiler_params=pltpu.CompilerParams(vmem_limit_bytes=VMEM_LIMIT),
+        name="update",
+    )(*results)
 
 
 def device_at(place, n):
@@ -24,7 +334,7 @@
     return jnp.where(place < half, up, down)
 
 
-def kernel(n, m, subs, max_norm, slow_hbm, fast_hbm, moment_hbm,
+def ring_kernel(n, m, subs, max_norm, slow_hbm, fast_hbm, moment_hbm,
            slow_out, moment_out, fast_out,
            ring, slow_ref, fast_ref, moment_ref, pseudo_ref, parts, norms, moment_sem, load_sem, send_sem, recv_sem,
            part_send, part_recv, norm_send, norm_recv):
@@ -232,24 +542,17 @@
     )(*arrays)
 
 
-def body(slow_weights, fast_weights, momentum):
-    n, m = lax.axis_size("dp"), lax.axis_size("mp")
-    layers, depth, cols = slow_weights.shape
-    rows = layers * depth
-    max_norm = CLIP_LEVEL * math.sqrt(rows * cols * m)
+def ring(n, m, max_norm, slow, fast, moment):
+    rows, cols = slow.shape
     subs = SUBS
     while rows % (n * subs * 16):
         subs -= 1
     sub = rows // (n * subs)
-    slow = slow_weights.reshape(rows, cols)
     hbm = pl.BlockSpec(memory_space=pltpu.HBM)
     vmem = pl.BlockSpec(memory_space=pltpu.VMEM)
-    flat = (slow_weights, fast_weights, momentum)
-    flat = [
-        pltpu.with_memory_space_constraint(x.reshape(rows, cols), pltpu.HBM) for x in flat
-    ]
+    flat = [pltpu.with_memory_space_constraint(x, pltpu.HBM) for x in (slow, fast, moment)]
     results = pl.pallas_call(
-        functools.partial(kernel, n, m, subs, max_norm),
+        functools.partial(ring_kernel, n, m, subs, max_norm),
         out_shape=(
             jax.ShapeDtypeStruct((rows, cols), jnp.float32),
             jax.ShapeDtypeStruct((rows, cols), jnp.float32),
@@ -279,7 +582,19 @@
         ),
         name="ring",
     )(*flat)
-    slow_next, momentum_next, fast_next = emit(results, 4)
+    return emit(results, 4)
+
+
+def body(slow_weights, fast_weights, momentum):
+    n, m = lax.axis_size("dp"), lax.axis_size("mp")
+    layers, depth, cols = slow_weights.shape
+    rows = layers * depth
+    max_norm = CLIP_LEVEL * math.sqrt(rows * cols * m)
+    flat = [x.reshape(rows, cols) for x in (slow_weights, fast_weights, momentum)]
+    groups = 1 + max(e[0] for e in OUTER + INNER) // 4
+    columns = n // 2
+    form = ladder if columns == 4 and rows % (groups * 4 * 16) == 0 else ring
+    slow_next, momentum_next, fast_next = form(n, m, max_norm, *flat)
     return (
         slow_next.reshape(slow_weights.shape),
         momentum_next.reshape(slow_weights.shape),

time: 81.9 us -> 75.4 us (0.921)
  Pallas kernels: 81.1 us -> 74.6 us
    pallas_call x2, Pallas kernels: 81.1 us -> 74.6 us  [the longest x1 70.7 us: ladder(): pl.pallas_call(functools.partial(ladder_kernel, n, m, max_norm), out_shap...]
where the time goes in v1:
time: 75.4 us; the launch traced here: 75.3 us
  Pallas kernels  74.6 us (99%)
    pallas_call x1, Pallas kernels, ladder(): pl.pallas_call(functools.partial(ladder_kernel, n, m, max_norm), out_shap...  70.7 us
    pallas_call x1, Pallas kernels, ladder(): pl.pallas_call(functools.partial(update_kernel, pieces), out_shape=(whole...  3.99 us

profile of v1, /device:TPU:0, one launch (start us, length us, event | category | flops | bytes accessed | tf_op | source)
XLA Modules:
  0.0 75.3 jit_solution(4992308401767016165)
XLA Ops:
  0.6 70.7 %ladder.1 = (f32[3584,256]{1,0:T(8,128)S(1)}, f32[3584,256]{1,0:T(8,128)S(1)}, f32[3584,256]{1,0:T(8,128)S(1)}, f32[8,128]{1,0:T(8,128)S(1)}) custom-call(f32[3584,256]{1,0:T(8,128)} %bitcast.6, bf16[3584,256]{1,0:T(8,128)(2,1)} %bitcast.8, f32[3584,256]{1,0:T(8,128)} %bitcast.7), custom_call_target="tpu_custom_call" | custom-call | tf_op jit(solution)/shard_map/ladder/pallas_call | solution.py:285
  71.3 4.0 %update.1 = (f32[3584,256]{1,0:T(8,128)}, f32[3584,256]{1,0:T(8,128)}, bf16[3584,256]{1,0:T(8,128)(2,1)}) custom-call(f32[3584,256]{1,0:T(8,128)S(1)} %get-tuple-element.10.pseudo, f32[3584,256]{1,0:T(8,128)S(1)} %get-tuple-element.11.slow_ref, f32[3584,256]{1,0:T(8,128)S(1)} %get-tuple-element.12.moment_ref, f32[8,128]{1,0:T(8,128)S(1)} %get-tuple-element.13.factor_ref), custom_call_target="tpu_custom_call" | custom-call | tf_op jit(solution)/shard_map/update/pallas_call | solution.py:314

commit v2 on v1

--- a/solution.py
+++ b/solution.py
@@ -17,47 +17,43 @@
 VMEM_LIMIT = 24 * 1024 * 1024
 LADDER_LIMIT = 40 * 1024 * 1024
 
+SIZES = (3, 7, 7, 7, 6, 3, 2, 4, 1, 7, 2, 7)
 OUTER = (
-    (3, 0, 1, 0), (11, 0, 4, 0), (7, 0, 4, 0), (51, 0, 1, 0), (2, 0, 1, 0), (9, 0, 4, 0),
-    (1, 0, 1, 0), (45, 0, 4, 0), (10, 4, 1, 0), (5, 1, 4, 0), (6, 4, 1, 0), (47, 1, 4, 0),
-    (0, 0, 1, 0), (41, 1, 4, 0), (8, 4, 1, 0), (53, 1, 4, 0), (4, 4, 1, 0), (43, 0, 4, 0),
-    (46, 4, 1, 0), (55, 0, 4, 0), (49, 0, 1, 0), (35, 1, 4, 0), (44, 4, 1, 0), (37, 1, 4, 0),
-    (50, 0, 1, 0), (21, 1, 4, 0), (48, 0, 1, 0), (33, 0, 4, 0), (42, 4, 1, 0), (31, 0, 4, 0),
-    (40, 4, 1, 0), (39, 0, 4, 0), (54, 4, 1, 0), (27, 1, 4, 0), (15, 0, 1, 0), (19, 0, 4, 0),
-    (34, 4, 1, 0), (23, 1, 4, 0), (52, 4, 1, 0), (29, 0, 4, 0), (32, 4, 1, 0), (6, 8, 32, 2),
-    (13, 0, 1, 0), (25, 0, 4, 0), (14, 0, 1, 0), (8, 8, 32, 2), (30, 4, 1, 0), (48, 8, 32, 2),
-    (26, 4, 1, 0), (4, 8, 32, 2), (12, 0, 1, 0), (46, 8, 32, 2), (28, 4, 1, 0), (50, 8, 32, 2),
-    (49, 8, 8, 2), (44, 8, 32, 2), (24, 4, 1, 0), (40, 8, 32, 2), (38, 4, 1, 0), (52, 8, 32, 2),
-    (22, 4, 1, 0), (42, 8, 32, 2), (18, 4, 1, 0), (54, 8, 32, 2), (17, 0, 1, 0), (34, 8, 32, 2),
-    (36, 4, 1, 0), (32, 8, 32, 2), (20, 4, 1, 0), (12, 8, 32, 2), (16, 0, 1, 0), (28, 8, 32, 2),
-    (24, 8, 32, 2), (30, 8, 32, 2), (13, 8, 8, 2), (26, 8, 32, 2), (36, 8, 32, 2), (31, 8, 8, 2),
-    (16, 8, 32, 2), (38, 8, 32, 2), (37, 8, 8, 2), (22, 8, 32, 2), (17, 8, 8, 2), (0, 8, 0, 2),
-    (2, 8, 0, 2), (1, 8, 0, 2), (10, 8, 0, 2), (3, 8, 0, 2), (11, 8, 0, 2), (7, 8, 0, 2),
-    (9, 8, 0, 2), (5, 8, 0, 2), (47, 8, 0, 2), (51, 8, 0, 2), (45, 8, 0, 2), (41, 8, 0, 2),
-    (53, 8, 0, 2), (43, 8, 0, 2), (14, 8, 0, 2), (55, 8, 0, 2), (35, 8, 0, 2), (33, 8, 0, 2),
-    (15, 8, 0, 2), (29, 8, 0, 2), (25, 8, 0, 2), (20, 8, 0, 2), (27, 8, 0, 2), (21, 8, 0, 2),
-    (39, 8, 0, 2), (18, 8, 0, 2), (23, 8, 0, 2), (19, 8, 0, 2),
+    (35, 0, 4, 0), (23, 0, 1, 0), (31, 0, 4, 0), (22, 0, 1, 0), (29, 0, 4, 0), (21, 0, 1, 0),
+    (33, 0, 4, 0), (43, 0, 1, 0), (11, 0, 4, 0), (34, 4, 1, 0), (20, 0, 1, 0), (30, 4, 1, 0),
+    (9, 0, 4, 0), (28, 4, 1, 0), (42, 0, 1, 0), (15, 0, 4, 0), (41, 0, 1, 0), (10, 4, 1, 0),
+    (13, 0, 4, 0), (40, 0, 1, 0), (27, 0, 1, 0), (3, 1, 4, 0), (26, 0, 1, 0), (14, 4, 1, 0),
+    (39, 0, 4, 0), (47, 0, 1, 0), (1, 1, 4, 0), (25, 0, 4, 0), (37, 1, 4, 0), (2, 4, 1, 0),
+    (38, 4, 1, 0), (19, 0, 4, 0), (46, 0, 1, 0), (7, 1, 4, 0), (5, 0, 1, 0), (17, 0, 4, 0),
+    (18, 4, 1, 0), (45, 0, 4, 0), (6, 4, 1, 0), (32, 5, 40, 1), (8, 5, 40, 1), (12, 5, 40, 1),
+    (0, 5, 40, 1), (24, 5, 40, 1), (36, 5, 40, 1), (44, 5, 40, 1), (16, 5, 40, 1), (34, 8, 32, 2),
+    (4, 1, 40, 1), (-1, 0, 0, 4), (10, 8, 32, 2), (35, 8, 8, 2), (-1, 0, 0, 5), (14, 8, 32, 2),
+    (5, 8, 8, 2), (2, 8, 32, 2), (11, 8, 8, 2), (26, 8, 32, 2), (38, 8, 32, 2), (15, 8, 8, 2),
+    (3, 8, 8, 2), (46, 8, 32, 2), (27, 8, 8, 2), (18, 8, 32, 2), (20, 8, 0, 2), (21, 8, 0, 2),
+    (28, 8, 0, 2), (22, 8, 0, 2), (23, 8, 0, 2), (30, 8, 0, 2), (29, 8, 0, 2), (40, 8, 0, 2),
+    (31, 8, 0, 2), (41, 8, 0, 2), (42, 8, 0, 2), (33, 8, 0, 2), (9, 8, 0, 2), (43, 8, 0, 2),
+    (13, 8, 0, 2), (1, 8, 0, 2), (25, 8, 0, 2), (37, 8, 0, 2), (45, 8, 0, 2), (17, 8, 0, 2),
+    (39, 8, 0, 2), (6, 8, 0, 2), (47, 8, 0, 2), (19, 8, 0, 2), (7, 8, 0, 2),
 )
 INNER = (
-    (5, 0, 1, 0), (47, 0, 1, 0), (9, 0, 4, 0), (11, 0, 4, 0), (41, 0, 1, 0), (7, 0, 4, 0),
-    (53, 0, 1, 0), (45, 0, 4, 0), (3, 1, 2, 0), (35, 0, 1, 0), (43, 0, 4, 0), (51, 1, 2, 0),
-    (27, 0, 1, 0), (55, 0, 4, 0), (2, 1, 2, 0), (37, 0, 1, 0), (33, 0, 4, 0), (21, 0, 1, 0),
-    (1, 3, 4, 0), (10, 5, 2, 0), (23, 0, 1, 0), (29, 0, 4, 0), (6, 5, 2, 0), (25, 0, 4, 0),
-    (0, 3, 4, 0), (0, 4, 24, 3), (8, 7, 56, 1), (4, 3, 56, 1), (46, 1, 2, 0), (31, 0, 4, 0),
-    (2, 8, 8, 2), (1, 4, 24, 3), (49, 3, 4, 0), (10, 8, 40, 2), (50, 1, 2, 0), (6, 8, 40, 2),
-    (44, 7, 56, 1), (3, 8, 8, 2), (42, 5, 2, 0), (39, 0, 4, 0), (48, 7, 24, 1), (19, 0, 4, 0),
-    (11, 8, 8, 2), (54, 5, 2, 0), (46, 8, 40, 2), (15, 1, 2, 0), (50, 8, 40, 2), (34, 1, 2, 0),
-    (40, 3, 56, 1), (52, 3, 56, 1), (32, 7, 56, 1), (13, 3, 4, 0), (14, 1, 2, 0), (42, 8, 40, 2),
-    (30, 5, 2, 0), (54, 8, 40, 2), (26, 1, 2, 0), (34, 8, 40, 2), (12, 7, 24, 1), (28, 7, 56, 1),
-    (14, 8, 40, 2), (24, 7, 56, 1), (30, 8, 8, 2), (38, 5, 2, 0), (22, 1, 2, 0), (15, 8, 8, 2),
-    (26, 8, 40, 2), (18, 5, 2, 0), (17, 1, 4, 0), (36, 3, 24, 1), (20, 3, 56, 1), (16, 7, 24, 1),
-    (-1, 0, 0, 4), (38, 8, 40, 2), (22, 8, 40, 2), (21, 8, 8, 2), (-1, 0, 0, 5), (18, 8, 40, 2),
-    (19, 8, 8, 2), (9, 8, 0, 2), (5, 8, 0, 2), (7, 8, 0, 2), (45, 8, 0, 2), (47, 8, 0, 2),
-    (51, 8, 0, 2), (41, 8, 0, 2), (53, 8, 0, 2), (33, 8, 0, 2), (43, 8, 0, 2), (49, 8, 0, 2),
-    (55, 8, 0, 2), (35, 8, 0, 2), (29, 8, 0, 2), (25, 8, 0, 2), (27, 8, 0, 2), (13, 8, 0, 2),
-    (39, 8, 0, 2), (23, 8, 0, 2), (31, 8, 0, 2), (37, 8, 0, 2), (17, 8, 0, 2),
+    (35, 0, 4, 0), (31, 0, 4, 0), (3, 0, 1, 0), (7, 0, 1, 0), (33, 0, 4, 0), (11, 0, 4, 0),
+    (1, 0, 1, 0), (23, 1, 2, 0), (29, 0, 4, 0), (37, 0, 1, 0), (22, 1, 2, 0), (15, 0, 4, 0),
+    (43, 1, 2, 0), (34, 5, 2, 0), (21, 3, 4, 0), (20, 3, 4, 0), (30, 5, 2, 0), (32, 6, 1, 0),
+    (9, 0, 4, 0), (42, 1, 2, 0), (20, 4, 24, 3), (39, 0, 4, 0), (21, 4, 24, 3), (28, 7, 56, 1),
+    (10, 5, 2, 0), (22, 8, 8, 2), (40, 3, 4, 0), (23, 8, 8, 2), (41, 3, 4, 0), (27, 1, 4, 0),
+    (30, 8, 8, 2), (13, 0, 4, 0), (14, 5, 2, 0), (29, 8, 24, 2), (19, 0, 4, 0), (8, 6, 1, 0),
+    (26, 5, 2, 0), (47, 1, 4, 0), (2, 1, 2, 0), (40, 4, 24, 3), (12, 6, 1, 0), (25, 0, 4, 0),
+    (38, 5, 2, 0), (45, 0, 4, 0), (31, 8, 8, 2), (41, 4, 24, 3), (-1, 0, 0, 4), (17, 0, 4, 0),
+    (42, 8, 8, 2), (46, 5, 2, 0), (0, 2, 1, 0), (36, 2, 1, 0), (-1, 0, 0, 5), (5, 1, 4, 0),
+    (18, 5, 2, 0), (43, 8, 8, 2), (24, 6, 1, 0), (44, 6, 1, 0), (6, 1, 2, 0), (32, 8, 48, 2),
+    (16, 6, 1, 0), (8, 8, 48, 2), (4, 6, 1, 0), (12, 8, 48, 2), (34, 8, 8, 2), (0, 8, 48, 2),
+    (10, 8, 8, 2), (24, 8, 48, 2), (36, 8, 48, 2), (14, 8, 8, 2), (2, 8, 8, 2), (44, 8, 48, 2),
+    (26, 8, 8, 2), (16, 8, 48, 2), (38, 8, 40, 2), (4, 8, 16, 2), (46, 8, 40, 2), (18, 8, 40, 2),
+    (5, 8, 16, 2), (6, 8, 8, 2), (7, 8, 8, 2), (33, 8, 0, 2), (9, 8, 0, 2), (13, 8, 0, 2),
+    (1, 8, 0, 2), (25, 8, 0, 2), (37, 8, 0, 2), (45, 8, 0, 2), (35, 8, 0, 2), (17, 8, 0, 2),
+    (39, 8, 0, 2), (11, 8, 0, 2), (47, 8, 0, 2), (15, 8, 0, 2), (19, 8, 0, 2), (3, 8, 0, 2),
+    (27, 8, 0, 2),
 )
-
 
 def ladder_kernel(n, m, max_norm, slow_hbm, fast_hbm, moment_hbm,
                   pseudo, slow_ref, moment_ref, factor_ref,
@@ -65,7 +61,9 @@
                   moment_sem, load_sem, send_sem, recv_sem, norm_send, norm_recv, part_send, part_recv):
     rows, cols = slow_ref.shape
     groups = load_sem.shape[1]
-    size = rows // (4 * groups)
+    unit = rows // (4 * sum(SIZES))
+    sizes = [unit * s for s in SIZES]
+    bases = [4 * sum(sizes[:g]) for g in range(groups)]
     half = n // 4
     me = lax.axis_index("dp")
     mine = lax.axis_index("mp")
@@ -79,10 +77,9 @@
     rung = 2 * z + 1 - y
     target = (near, across, rung)
     spots = [(far + upper - 2 * far * upper) * 2 + (other + y - 2 * other * y) for far in range(2) for other in range(2)]
-    block = size * 4
 
     def load(g):
-        at = pl.ds(g * block, block)
+        at = pl.ds(bases[g], 4 * sizes[g])
         return (
             pltpu.make_async_copy(slow_hbm.at[at], slow_ref.at[at], load_sem.at[0, g]),
             pltpu.make_async_copy(fast_hbm.at[at], fast_ref.at[at], load_sem.at[1, g]),
@@ -114,23 +111,23 @@
     moment_load.start()
     square[...] = jnp.zeros_like(square)
 
-    def place(chunk):
-        return (chunk // 4) * 4 + spots[chunk % 4]
-
-    def at_of(spot):
-        return pl.ds(pl.multiple_of(spot * size, size), size)
-
-    def sum_copy(spot, k):
-        at = at_of(spot)
-        return pltpu.make_async_remote_copy(
-            src_ref=part.at[at], dst_ref=inbox.at[k, at], send_sem=send_sem, recv_sem=recv_sem.at[k, spot],
+    def at_of(chunk):
+        g = chunk // 4
+        return pl.ds(pl.multiple_of(bases[g] + spots[chunk % 4] * sizes[g], 16), sizes[g])
+
+    def sum_copy(chunk, k):
+        at = at_of(chunk)
+        return pltpu.make_async_remote_copy(
+            src_ref=part.at[at], dst_ref=inbox.at[k, at], send_sem=send_sem,
+            recv_sem=recv_sem.at[k, chunk // 4 * 4 + spots[chunk % 4]],
             device_id={"dp": target[k]}, device_id_type=MESH,
         )
 
-    def mean_copy(spot, k):
-        at = at_of(spot)
-        return pltpu.make_async_remote_copy(
-            src_ref=pseudo.at[at], dst_ref=pseudo.at[at], send_sem=send_sem, recv_sem=recv_sem.at[3, spot],
+    def mean_copy(chunk, k):
+        at = at_of(chunk)
+        return pltpu.make_async_remote_copy(
+            src_ref=pseudo.at[at], dst_ref=pseudo.at[at], send_sem=send_sem,
+            recv_sem=recv_sem.at[3, chunk // 4 * 4 + spots[chunk % 4]],
             device_id={"dp": target[k]}, device_id_type=MESH,
         )
 
@@ -142,17 +139,9 @@
 
     def part_copy(k):
         return pltpu.make_async_remote_copy(
-            src_ref=parts.at[me], dst_ref=parts.at[me], send_sem=part_send.at[k], recv_sem=part_recv.at[me],
+            src_ref=parts.at[me], dst_ref=parts.at[me], send_sem=part_send.at[k], recv_sem=part_recv.at[k],
             device_id={"dp": lax.rem(me + k, n)}, device_id_type=MESH,
         )
-
-    roots = [2 * q + c for q in (half - 1, half) for c in range(2)]
-
-    def part_wait(j):
-        pltpu.make_async_remote_copy(
-            src_ref=parts.at[j], dst_ref=parts.at[j], send_sem=part_send.at[0], recv_sem=part_recv.at[j],
-            device_id={"dp": lax.rem(me + 1, n)}, device_id_type=MESH,
-        ).wait_recv()
 
     def run(steps):
         seen = set()
@@ -178,13 +167,12 @@
                 seen.add(g)
                 for copy in load(g):
                     copy.wait()
-            spot = place(chunk)
-            at = at_of(spot)
+            at = at_of(chunk)
             for k in range(3):
                 if waits >> k & 1:
-                    sum_copy(spot, k).wait_recv()
+                    sum_copy(chunk, k).wait_recv()
             if waits & 8:
-                mean_copy(spot, 2).wait_recv()
+                mean_copy(chunk, 2).wait_recv()
             if kind in (0, 1, 3):
                 value = part[at] if kind == 3 else slow_ref[at] - fast_ref[at].astype(jnp.float32)
                 for k in range(3):
@@ -197,44 +185,37 @@
                     pseudo[at] = value
             for k in (1, 0, 2):
                 if sends >> k & 1:
-                    sum_copy(spot, k).start()
-                    sent += 1
+                    sum_copy(chunk, k).start()
+                    sent += sizes[g]
                 if sends >> (3 + k) & 1:
-                    mean_copy(spot, k).start()
-                    sent += 1
+                    mean_copy(chunk, k).start()
+                    sent += sizes[g]
             if kind in (1, 3):
                 weight = 1.0 if kind == 1 else 0.5
-                square[...] += weight * jnp.sum((value * value).reshape(size // 8, 8, cols), axis=0)
+                square[...] += weight * jnp.sum((value * value).reshape(sizes[g] // 8, 8, cols), axis=0)
         for g in loads:
             if g not in seen:
                 for copy in load(g):
                     copy.wait()
-        whole = inbox.reshape(3 * rows, cols).at[pl.ds(0, sent * size)]
+        whole = inbox.reshape(3 * rows, cols).at[pl.ds(0, sent)]
         pltpu.make_async_copy(whole, whole, send_sem).wait()
 
     @pl.when(outer)
     def _():
         pl.semaphore_wait(barrier, m + 1)
         run(OUTER)
-        for j in roots:
-            part_wait(j)
 
     @pl.when(jnp.logical_not(outer))
     def _():
         pl.semaphore_wait(barrier, m + 2)
         run(INNER)
-        for k in range(1, m):
-            norm_copy(k).wait_send()
-        for k in range(1, n):
-            part_copy(k).wait_send()
-        for j in roots:
-
-            @pl.when(me != j)
-            def _():
-                part_wait(j)
-
-    total = parts[roots[0]]
-    for j in roots[1:]:
+
+    for k in range(1, m):
+        norm_copy(k).wait_send()
+    for k in range(1, n):
+        part_copy(k).wait()
+    total = parts[0]
+    for j in range(1, n):
         total = total + parts[j]
     total = jnp.sum(jnp.sum(total, axis=1, keepdims=True), axis=0, keepdims=True)
     factor = jnp.minimum(1.0, max_norm / (jnp.sqrt(total) + EPSILON))
@@ -276,7 +257,7 @@
 
 def ladder(n, m, max_norm, slow, fast, moment):
     rows, cols = slow.shape
-    groups = 1 + max(e[0] for e in OUTER + INNER) // 4
+    groups = len(SIZES)
     hbm = pl.BlockSpec(memory_space=pltpu.HBM)
     vmem = pl.BlockSpec(memory_space=pltpu.VMEM)
     whole = jax.ShapeDtypeStruct((rows, cols), jnp.float32)
@@ -591,9 +572,8 @@
     rows = layers * depth
     max_norm = CLIP_LEVEL * math.sqrt(rows * cols * m)
     flat = [x.reshape(rows, cols) for x in (slow_weights, fast_weights, momentum)]
-    groups = 1 + max(e[0] for e in OUTER + INNER) // 4
     columns = n // 2
-    form = ladder if columns == 4 and rows % (groups * 4 * 16) == 0 else ring
+    form = ladder if columns == 4 and rows % (sum(SIZES) * 4 * 16) == 0 else ring
     slow_next, momentum_next, fast_next = form(n, m, max_norm, *flat)
     return (
         slow_next.reshape(slow_weights.shape),

time: 75.4 us -> 73.9 us (0.980)
  Pallas kernels: 74.6 us -> 73.1 us
    pallas_call x1, Pallas kernels: 70.7 us -> 69.1 us  [ladder(): pl.pallas_call(functools.partial(ladder_kernel, n, m, max_norm), out_shap...]
where the time goes in v2:
time: 73.9 us; the launch traced here: 73.7 us
  Pallas kernels  73.1 us (99%)
    pallas_call x1, Pallas kernels, ladder(): pl.pallas_call(functools.partial(ladder_kernel, n, m, max_norm), out_shap...  69.1 us
    pallas_call x1, Pallas kernels, ladder(): pl.pallas_call(functools.partial(update_kernel, pieces), out_shape=(whole...  3.99 us

profile of v2, /device:TPU:0, one launch (start us, length us, event | category | flops | bytes accessed | tf_op | source)
XLA Modules:
  0.0 73.7 jit_solution(13241967219915843378)
XLA Ops:
  0.6 69.1 %ladder.1 = (f32[3584,256]{1,0:T(8,128)S(1)}, f32[3584,256]{1,0:T(8,128)S(1)}, f32[3584,256]{1,0:T(8,128)S(1)}, f32[8,128]{1,0:T(8,128)S(1)}) custom-call(f32[3584,256]{1,0:T(8,128)} %bitcast.6, bf16[3584,256]{1,0:T(8,128)(2,1)} %bitcast.8, f32[3584,256]{1,0:T(8,128)} %bitcast.7), custom_call_target="tpu_custom_call" | custom-call | tf_op jit(solution)/shard_map/ladder/pallas_call | solution.py:266
  69.7 4.0 %update.1 = (f32[3584,256]{1,0:T(8,128)}, f32[3584,256]{1,0:T(8,128)}, bf16[3584,256]{1,0:T(8,128)(2,1)}) custom-call(f32[3584,256]{1,0:T(8,128)S(1)} %get-tuple-element.10.pseudo, f32[3584,256]{1,0:T(8,128)S(1)} %get-tuple-element.11.slow_ref, f32[3584,256]{1,0:T(8,128)S(1)} %get-tuple-element.12.moment_ref, f32[8,128]{1,0:T(8,128)S(1)} %get-tuple-element.13.factor_ref), custom_call_target="tpu_custom_call" | custom-call | tf_op jit(solution)/shard_map/update/pallas_call | solution.py:295

commit v3 on v2

--- a/solution.py
+++ b/solution.py
@@ -56,8 +56,8 @@
 )
 
 def ladder_kernel(n, m, max_norm, slow_hbm, fast_hbm, moment_hbm,
-                  pseudo, slow_ref, moment_ref, factor_ref,
-                  fast_ref, part, inbox, square, norms, parts,
+                  slow_new, moment_new, fast_new,
+                  pseudo, slow_ref, moment_ref, fast_ref, part, inbox, square, norms, parts,
                   moment_sem, load_sem, send_sem, recv_sem, norm_send, norm_recv, part_send, part_recv):
     rows, cols = slow_ref.shape
     groups = load_sem.shape[1]
@@ -143,10 +143,31 @@
             device_id={"dp": lax.rem(me + k, n)}, device_id_type=MESH,
         )
 
+    def clip():
+        for k in range(1, n):
+            part_copy(k).wait_recv()
+        total = parts[0]
+        for j in range(1, n):
+            total = total + parts[j]
+        total = jnp.sum(jnp.sum(total, axis=1, keepdims=True), axis=0, keepdims=True)
+        moment_load.wait()
+        return jnp.minimum(1.0, max_norm / (jnp.sqrt(total) + EPSILON))
+
+    def update(factor, chunk):
+        at = at_of(chunk)
+        gradient = factor * pseudo[at]
+        moment = MOMENTUM_RATE * moment_ref[at] + gradient
+        slow = slow_ref[at] - OUTER_RATE * (gradient + MOMENTUM_RATE * moment)
+        moment_new[at] = moment
+        slow_new[at] = slow
+        fast_new[at] = slow.astype(fast_new.dtype)
+
     def run(steps):
         seen = set()
         sent = 0
-        for chunk, waits, sends, kind in steps:
+        last = max(i for i, step in enumerate(steps) if step[2] or step[3] > 2)
+        ready = []
+        for index, (chunk, waits, sends, kind) in enumerate(steps):
             if kind == 4:
                 norms[mine] = square[:, : cols // 2] + square[:, cols // 2 :]
                 for k in range(1, m):
@@ -193,10 +214,18 @@
             if kind in (1, 3):
                 weight = 1.0 if kind == 1 else 0.5
                 square[...] += weight * jnp.sum((value * value).reshape(sizes[g] // 8, 8, cols), axis=0)
-        for g in loads:
-            if g not in seen:
-                for copy in load(g):
-                    copy.wait()
+            if waits & 8 or kind in (1, 3):
+                ready.append(chunk)
+            if index == last:
+                factor = clip()
+                for g in loads:
+                    if g not in seen:
+                        for copy in load(g):
+                            copy.wait()
+            if index >= last:
+                for other in ready:
+                    update(factor, other)
+                ready.clear()
         whole = inbox.reshape(3 * rows, cols).at[pl.ds(0, sent)]
         pltpu.make_async_copy(whole, whole, send_sem).wait()
 
@@ -213,46 +242,7 @@
     for k in range(1, m):
         norm_copy(k).wait_send()
     for k in range(1, n):
-        part_copy(k).wait()
-    total = parts[0]
-    for j in range(1, n):
-        total = total + parts[j]
-    total = jnp.sum(jnp.sum(total, axis=1, keepdims=True), axis=0, keepdims=True)
-    factor = jnp.minimum(1.0, max_norm / (jnp.sqrt(total) + EPSILON))
-    factor_ref[...] = jnp.broadcast_to(factor, factor_ref.shape)
-    moment_load.wait()
-
-
-def update_kernel(pieces, pseudo, slow_ref, moment_ref, factor_ref,
-                  slow_out, moment_out, fast_out, slow_new, moment_new, fast_new, sem):
-    rows, cols = slow_ref.shape
-    size = rows // pieces
-    factor = factor_ref[0:1, 0:1]
-
-    def copies(k):
-        at = pl.ds(pl.multiple_of(k * size, size), size)
-        pairs = ((slow_new, slow_out), (moment_new, moment_out), (fast_new, fast_out))
-        return [pltpu.make_async_copy(a.at[at], b.at[at], sem.at[i, k]) for i, (a, b) in enumerate(pairs)]
-
-    def piece(k, carry):
-        at = pl.ds(pl.multiple_of(k * size, size), size)
-        gradient = factor * pseudo[at]
-        moment = MOMENTUM_RATE * moment_ref[at] + gradient
-        slow = slow_ref[at] - OUTER_RATE * (gradient + MOMENTUM_RATE * moment)
-        moment_new[at] = moment
-        slow_new[at] = slow
-        fast_new[at] = slow.astype(fast_new.dtype)
-        for copy in copies(k):
-            copy.start()
-        return carry
-
-    def finish(k, carry):
-        for copy in copies(k):
-            copy.wait()
-        return carry
-
-    lax.fori_loop(0, pieces, piece, 0)
-    lax.fori_loop(0, pieces, finish, 0)
+        part_copy(k).wait_send()
 
 
 def ladder(n, m, max_norm, slow, fast, moment):
@@ -265,10 +255,13 @@
     flat = [pltpu.with_memory_space_constraint(x, pltpu.HBM) for x in (slow, fast, moment)]
     results = pl.pallas_call(
         functools.partial(ladder_kernel, n, m, max_norm),
-        out_shape=(whole, whole, whole, jax.ShapeDtypeStruct((8, 128), jnp.float32)),
+        out_shape=(whole, whole, jax.ShapeDtypeStruct((rows, cols), fast.dtype)),
         in_specs=[hbm, hbm, hbm],
-        out_specs=(vmem, vmem, vmem, vmem),
+        out_specs=(vmem, vmem, vmem),
         scratch_shapes=[
+            pltpu.VMEM((rows, cols), jnp.float32),
+            pltpu.VMEM((rows, cols), jnp.float32),
+            pltpu.VMEM((rows, cols), jnp.float32),
             pltpu.VMEM((rows, cols), fast.dtype),
             pltpu.VMEM((rows, cols), jnp.float32),
             pltpu.VMEM((3, rows, cols), jnp.float32),
@@ -289,23 +282,7 @@
         ),
         name="ladder",
     )(*flat)
-    pieces = 14
-    while rows % (pieces * 16):
-        pieces -= 1
-    return pl.pallas_call(
-        functools.partial(update_kernel, pieces),
-        out_shape=(whole, whole, jax.ShapeDtypeStruct((rows, cols), fast.dtype)),
-        in_specs=[vmem] * 4,
-        out_specs=(hbm, hbm, hbm),
-        scratch_shapes=[
-            pltpu.VMEM((rows, cols), jnp.float32),
-            pltpu.VMEM((rows, cols), jnp.float32),
-            pltpu.VMEM((rows, cols), fast.dtype),
-            dma((3, pieces)),
-        ],
-        compiler_params=pltpu.CompilerParams(vmem_limit_bytes=VMEM_LIMIT),
-        name="update",
-    )(*results)
+    return emit(results, 4)
 
 
 def device_at(place, n):

time: 73.9 us -> 73.4 us (level)
  no operation moved by 1% of the time
where the time goes in v3:
time: 73.4 us; the launch traced here: 73.3 us
  Pallas kernels  72.6 us (99%)
    pallas_call x1, Pallas kernels, ladder(): pl.pallas_call(functools.partial(ladder_kernel, n, m, max_norm), out_shap...  69 us
    pallas_call x1, Pallas kernels, emit(): pl.pallas_call(functools.partial(emit_kernel, pieces), out_shape=tuple((j...  3.63 us

profile of v3, /device:TPU:0, one launch (start us, length us, event | category | flops | bytes accessed | tf_op | source)
XLA Modules:
  0.0 73.3 jit_solution(9498562582516828904)
XLA Ops:
  0.6 69.0 %ladder.1 = (f32[3584,256]{1,0:T(8,128)S(1)}, f32[3584,256]{1,0:T(8,128)S(1)}, bf16[3584,256]{1,0:T(8,128)(2,1)S(1)}) custom-call(f32[3584,256]{1,0:T(8,128)} %bitcast.6, bf16[3584,256]{1,0:T(8,128)(2,1)} %bitcast.8, f32[3584,256]{1,0:T(8,128)} %bitcast.7), custom_call_target="tpu_custom_call" | custom-call | tf_op jit(solution)/shard_map/ladder/pallas_call | solution.py:256
  69.7 3.6 %emit.1 = (f32[3584,256]{1,0:T(8,128)}, f32[3584,256]{1,0:T(8,128)}, bf16[3584,256]{1,0:T(8,128)(2,1)}) custom-call(f32[3584,256]{1,0:T(8,128)S(1)} %get-tuple-element.9.refs_0_, f32[3584,256]{1,0:T(8,128)S(1)} %get-tuple-element.10.refs_1_, bf16[3584,256]{1,0:T(8,128)(2,1)S(1)} %get-tuple-element.11.refs_2_), custom_call_target="tpu_custom_call" | custom-call | tf_op jit(solution)/shard_map/emit/pallas_call | solution.py:492

commit v4 on v3

--- a/solution.py
+++ b/solution.py
@@ -17,42 +17,34 @@
 VMEM_LIMIT = 24 * 1024 * 1024
 LADDER_LIMIT = 40 * 1024 * 1024
 
-SIZES = (3, 7, 7, 7, 6, 3, 2, 4, 1, 7, 2, 7)
+SIZES = (7, 3, 5, 7, 6, 7, 6, 8, 7)
 OUTER = (
-    (35, 0, 4, 0), (23, 0, 1, 0), (31, 0, 4, 0), (22, 0, 1, 0), (29, 0, 4, 0), (21, 0, 1, 0),
-    (33, 0, 4, 0), (43, 0, 1, 0), (11, 0, 4, 0), (34, 4, 1, 0), (20, 0, 1, 0), (30, 4, 1, 0),
-    (9, 0, 4, 0), (28, 4, 1, 0), (42, 0, 1, 0), (15, 0, 4, 0), (41, 0, 1, 0), (10, 4, 1, 0),
-    (13, 0, 4, 0), (40, 0, 1, 0), (27, 0, 1, 0), (3, 1, 4, 0), (26, 0, 1, 0), (14, 4, 1, 0),
-    (39, 0, 4, 0), (47, 0, 1, 0), (1, 1, 4, 0), (25, 0, 4, 0), (37, 1, 4, 0), (2, 4, 1, 0),
-    (38, 4, 1, 0), (19, 0, 4, 0), (46, 0, 1, 0), (7, 1, 4, 0), (5, 0, 1, 0), (17, 0, 4, 0),
-    (18, 4, 1, 0), (45, 0, 4, 0), (6, 4, 1, 0), (32, 5, 40, 1), (8, 5, 40, 1), (12, 5, 40, 1),
-    (0, 5, 40, 1), (24, 5, 40, 1), (36, 5, 40, 1), (44, 5, 40, 1), (16, 5, 40, 1), (34, 8, 32, 2),
-    (4, 1, 40, 1), (-1, 0, 0, 4), (10, 8, 32, 2), (35, 8, 8, 2), (-1, 0, 0, 5), (14, 8, 32, 2),
-    (5, 8, 8, 2), (2, 8, 32, 2), (11, 8, 8, 2), (26, 8, 32, 2), (38, 8, 32, 2), (15, 8, 8, 2),
-    (3, 8, 8, 2), (46, 8, 32, 2), (27, 8, 8, 2), (18, 8, 32, 2), (20, 8, 0, 2), (21, 8, 0, 2),
-    (28, 8, 0, 2), (22, 8, 0, 2), (23, 8, 0, 2), (30, 8, 0, 2), (29, 8, 0, 2), (40, 8, 0, 2),
-    (31, 8, 0, 2), (41, 8, 0, 2), (42, 8, 0, 2), (33, 8, 0, 2), (9, 8, 0, 2), (43, 8, 0, 2),
-    (13, 8, 0, 2), (1, 8, 0, 2), (25, 8, 0, 2), (37, 8, 0, 2), (45, 8, 0, 2), (17, 8, 0, 2),
-    (39, 8, 0, 2), (6, 8, 0, 2), (47, 8, 0, 2), (19, 8, 0, 2), (7, 8, 0, 2),
+    (3, 0, 4, 0), (15, 0, 1, 0), (7, 0, 1, 0), (11, 0, 4, 0), (14, 0, 1, 0), (1, 0, 4, 0),
+    (6, 0, 1, 0), (19, 0, 4, 0), (2, 4, 1, 0), (9, 0, 4, 0), (10, 4, 1, 0), (17, 0, 4, 0),
+    (0, 4, 1, 0), (31, 0, 4, 0), (18, 4, 1, 0), (35, 1, 4, 0), (29, 0, 1, 0), (13, 1, 4, 0),
+    (16, 4, 1, 0), (5, 1, 4, 0), (30, 4, 1, 0), (27, 1, 4, 0), (33, 1, 4, 0), (23, 0, 1, 0),
+    (21, 0, 4, 0), (4, 5, 8, 1), (34, 4, 1, 0), (25, 1, 4, 0), (22, 0, 1, 0), (12, 5, 40, 1),
+    (16, 8, 32, 2), (26, 4, 1, 0), (8, 5, 40, 1), (18, 8, 32, 2), (24, 4, 1, 0), (28, 1, 40, 1),
+    (6, 8, 32, 2), (32, 5, 40, 1), (20, 5, 40, 1), (-1, 0, 0, 4), (14, 8, 32, 2), (-1, 0, 0, 5),
+    (24, 8, 32, 2), (21, 8, 8, 2), (10, 8, 32, 2), (15, 8, 8, 2), (26, 8, 32, 2), (30, 8, 32, 2),
+    (11, 8, 8, 2), (34, 8, 32, 2), (0, 8, 0, 2), (2, 8, 0, 2), (1, 8, 0, 2), (3, 8, 0, 2),
+    (13, 8, 0, 2), (17, 8, 0, 2), (9, 8, 0, 2), (5, 8, 0, 2), (19, 8, 0, 2), (29, 8, 0, 2),
+    (7, 8, 0, 2), (33, 8, 0, 2), (25, 8, 0, 2), (27, 8, 0, 2), (22, 8, 0, 2), (31, 8, 0, 2),
+    (35, 8, 0, 2), (23, 8, 0, 2),
 )
 INNER = (
-    (35, 0, 4, 0), (31, 0, 4, 0), (3, 0, 1, 0), (7, 0, 1, 0), (33, 0, 4, 0), (11, 0, 4, 0),
-    (1, 0, 1, 0), (23, 1, 2, 0), (29, 0, 4, 0), (37, 0, 1, 0), (22, 1, 2, 0), (15, 0, 4, 0),
-    (43, 1, 2, 0), (34, 5, 2, 0), (21, 3, 4, 0), (20, 3, 4, 0), (30, 5, 2, 0), (32, 6, 1, 0),
-    (9, 0, 4, 0), (42, 1, 2, 0), (20, 4, 24, 3), (39, 0, 4, 0), (21, 4, 24, 3), (28, 7, 56, 1),
-    (10, 5, 2, 0), (22, 8, 8, 2), (40, 3, 4, 0), (23, 8, 8, 2), (41, 3, 4, 0), (27, 1, 4, 0),
-    (30, 8, 8, 2), (13, 0, 4, 0), (14, 5, 2, 0), (29, 8, 24, 2), (19, 0, 4, 0), (8, 6, 1, 0),
-    (26, 5, 2, 0), (47, 1, 4, 0), (2, 1, 2, 0), (40, 4, 24, 3), (12, 6, 1, 0), (25, 0, 4, 0),
-    (38, 5, 2, 0), (45, 0, 4, 0), (31, 8, 8, 2), (41, 4, 24, 3), (-1, 0, 0, 4), (17, 0, 4, 0),
-    (42, 8, 8, 2), (46, 5, 2, 0), (0, 2, 1, 0), (36, 2, 1, 0), (-1, 0, 0, 5), (5, 1, 4, 0),
-    (18, 5, 2, 0), (43, 8, 8, 2), (24, 6, 1, 0), (44, 6, 1, 0), (6, 1, 2, 0), (32, 8, 48, 2),
-    (16, 6, 1, 0), (8, 8, 48, 2), (4, 6, 1, 0), (12, 8, 48, 2), (34, 8, 8, 2), (0, 8, 48, 2),
-    (10, 8, 8, 2), (24, 8, 48, 2), (36, 8, 48, 2), (14, 8, 8, 2), (2, 8, 8, 2), (44, 8, 48, 2),
-    (26, 8, 8, 2), (16, 8, 48, 2), (38, 8, 40, 2), (4, 8, 16, 2), (46, 8, 40, 2), (18, 8, 40, 2),
-    (5, 8, 16, 2), (6, 8, 8, 2), (7, 8, 8, 2), (33, 8, 0, 2), (9, 8, 0, 2), (13, 8, 0, 2),
-    (1, 8, 0, 2), (25, 8, 0, 2), (37, 8, 0, 2), (45, 8, 0, 2), (35, 8, 0, 2), (17, 8, 0, 2),
-    (39, 8, 0, 2), (11, 8, 0, 2), (47, 8, 0, 2), (15, 8, 0, 2), (19, 8, 0, 2), (3, 8, 0, 2),
-    (27, 8, 0, 2),
+    (3, 0, 4, 0), (1, 0, 4, 0), (35, 0, 1, 0), (33, 0, 1, 0), (11, 0, 4, 0), (27, 0, 1, 0),
+    (19, 0, 4, 0), (15, 1, 2, 0), (25, 0, 1, 0), (7, 1, 2, 0), (9, 0, 4, 0), (17, 0, 4, 0),
+    (14, 1, 2, 0), (6, 1, 2, 0), (13, 2, 1, 0), (31, 0, 4, 0), (5, 2, 1, 0), (2, 5, 2, 0),
+    (21, 0, 4, 0), (12, 2, 1, 0), (10, 5, 2, 0), (4, 2, 1, 0), (0, 7, 56, 1), (18, 5, 2, 0),
+    (8, 6, 1, 0), (29, 1, 4, 0), (2, 8, 8, 2), (1, 8, 24, 2), (16, 7, 56, 1), (30, 5, 2, 0),
+    (3, 8, 8, 2), (23, 1, 4, 0), (18, 8, 40, 2), (4, 8, 48, 2), (34, 1, 2, 0), (28, 6, 1, 0),
+    (6, 8, 40, 2), (22, 5, 2, 0), (5, 8, 8, 2), (32, 2, 1, 0), (12, 8, 48, 2), (26, 1, 2, 0),
+    (20, 6, 1, 0), (8, 8, 48, 2), (14, 8, 8, 2), (24, 3, 56, 1), (-1, 0, 0, 4), (10, 8, 8, 2),
+    (28, 8, 48, 2), (-1, 0, 0, 5), (26, 8, 40, 2), (32, 8, 48, 2), (20, 8, 16, 2), (30, 8, 40, 2),
+    (34, 8, 40, 2), (21, 8, 16, 2), (22, 8, 8, 2), (23, 8, 8, 2), (17, 8, 0, 2), (19, 8, 0, 2),
+    (7, 8, 0, 2), (13, 8, 0, 2), (9, 8, 0, 2), (25, 8, 0, 2), (29, 8, 0, 2), (27, 8, 0, 2),
+    (33, 8, 0, 2), (15, 8, 0, 2), (31, 8, 0, 2), (11, 8, 0, 2), (35, 8, 0, 2),
 )
 
 def ladder_kernel(n, m, max_norm, slow_hbm, fast_hbm, moment_hbm,

time: 73.4 us -> 73.6 us (level)
  no operation moved by 1% of the time
where the time goes in v4:
time: 73.6 us; the launch traced here: 73.5 us
  Pallas kernels  72.8 us (99%)
    pallas_call x1, Pallas kernels, ladder(): pl.pallas_call(functools.partial(ladder_kernel, n, m, max_norm), out_shap...  69.2 us
    pallas_call x1, Pallas kernels, emit(): pl.pallas_call(functools.partial(emit_kernel, pieces), out_shape=tuple((j...  3.63 us

profile of v4, /device:TPU:0, one launch (start us, length us, event | category | flops | bytes accessed | tf_op | source)
XLA Modules:
  0.0 73.5 jit_solution(7422341023494256578)
XLA Ops:
  0.6 69.2 %ladder.1 = (f32[3584,256]{1,0:T(8,128)S(1)}, f32[3584,256]{1,0:T(8,128)S(1)}, bf16[3584,256]{1,0:T(8,128)(2,1)S(1)}) custom-call(f32[3584,256]{1,0:T(8,128)} %bitcast.6, bf16[3584,256]{1,0:T(8,128)(2,1)} %bitcast.8, f32[3584,256]{1,0:T(8,128)} %bitcast.7), custom_call_target="tpu_custom_call" | custom-call | tf_op jit(solution)/shard_map/ladder/pallas_call | solution.py:248
  69.8 3.6 %emit.1 = (f32[3584,256]{1,0:T(8,128)}, f32[3584,256]{1,0:T(8,128)}, bf16[3584,256]{1,0:T(8,128)(2,1)}) custom-call(f32[3584,256]{1,0:T(8,128)S(1)} %get-tuple-element.9.refs_0_, f32[3584,256]{1,0:T(8,128)S(1)} %get-tuple-element.10.refs_1_, bf16[3584,256]{1,0:T(8,128)(2,1)S(1)} %get-tuple-element.11.refs_2_), custom_call_target="tpu_custom_call" | custom-call | tf_op jit(solution)/shard_map/emit/pallas_call | solution.py:484
